TPU v7x, 32 devices: a whole 2x2x4 slice. The times are simulated.
32 devices in a mesh: emb: 8 (over z, x), seq: 4 (over y, core).
Axes of the slice: x: 2, y: 2, z: 4, core: 2. Of those that a mesh axis runs over, the one named last changes fastest.
Arguments:
- item_table: bfloat16 [32768, 512], P('emb'), may hold values from -6 to 6
- fetch_rows: int32 [8, 4, 8, 64], P('emb', 'seq'), may hold values from 0 to 4095
- event_slot: int32 [32768], P(('emb', 'seq')), may hold values from 0 to 511, as said below
- lengths: int32 [32, 8], P(('emb', 'seq')), may hold values from 1 to 512, 1024 in all within a row
- in_weight: bfloat16 [512, 2048], replicated, may hold values from -0.25 to 0.25
- out_weight: bfloat16 [512, 512], replicated, may hold values from -0.25 to 0.25
- out_grad: bfloat16 [32768, 512], P(('emb', 'seq')), may hold values from -6 to 6
Outputs:
- layer_out: bfloat16 [32768, 512], P(('emb', 'seq'))
- table_grad: float32 [32768, 512], P(('emb', 'seq'))
- in_weight_grad: float32 [512, 2048], replicated
- out_weight_grad: float32 [512, 512], replicated
Inputs may be any that keep to these rules, and one draw needn't show every extreme that they name: `event_slot`: within each buffer of 1024 events every slot 0 to 511 is named by at least one event.
All inputs are finite; a program needn't handle non-finite values.
Results may differ from a plain program's by a relative error of at most 0.02.
Values may be sent and summed in bfloat16 or wider, within the bound.
No kernel may reach another device: no remote copies, remote signals or barrier semaphores. Data moves between devices by JAX's collectives and lax.ppermute only.
A program may use at most 192 MiB of HBM per device.

v0:
```python
import jax
import jax.numpy as jnp
from jax import lax
from jax.sharding import PartitionSpec as P

HEADS = 4
MOST = 512
EPS = 1e-05


def normalize(rows_in):
    center = rows_in - jnp.mean(rows_in, axis=-1, keepdims=True)
    spread = jnp.mean(center * center, axis=-1, keepdims=True)
    return center * lax.rsqrt(spread + EPS)


def hstu_layer(events, in_weight, out_weight, lengths_row):
    rows_count, model_width = events.shape
    head_size = model_width // HEADS
    normed = normalize(events.astype(jnp.float32)).astype(jnp.bfloat16)
    hidden = jax.nn.silu(jnp.dot(normed, in_weight, preferred_element_type=jnp.float32))
    update_gate = hidden[:, :model_width]
    values = (
        hidden[:, model_width : 2 * model_width]
        .astype(jnp.bfloat16)
        .reshape(rows_count, HEADS, head_size)
    )
    queries = (
        hidden[:, 2 * model_width : 3 * model_width]
        .astype(jnp.bfloat16)
        .reshape(rows_count, HEADS, head_size)
    )
    key_rows = (
        hidden[:, 3 * model_width :].astype(jnp.bfloat16).reshape(rows_count, HEADS, head_size)
    )
    scores = jnp.einsum(
        "ihd,jhd->hij", queries, key_rows, preferred_element_type=jnp.float32
    ) * head_size ** (-0.5)
    places = jnp.arange(rows_count, dtype=jnp.int32)
    seq_ends = jnp.cumsum(lengths_row)
    segment = jnp.sum((places[:, None] >= seq_ends[None, :]).astype(jnp.int32), axis=1)
    allowed = (segment[:, None] == segment[None, :]) & (places[None, :] <= places[:, None])
    weights = jnp.where(allowed[None], jax.nn.silu(scores) / MOST, 0.0).astype(jnp.bfloat16)
    attended = jnp.einsum(
        "hij,jhd->ihd", weights, values, preferred_element_type=jnp.float32
    ).reshape(rows_count, model_width)
    gated_rows = (normalize(attended) * update_gate).astype(jnp.bfloat16)
    return (
        jnp.dot(gated_rows, out_weight, preferred_element_type=jnp.float32)
        + events.astype(jnp.float32)
    ).astype(jnp.bfloat16)


def on_device(item_table, fetch_rows, event_slot, lengths, in_weight, out_weight, out_grad):
    emb_count = lax.axis_size("emb")
    seq_count = lax.axis_size("seq")
    model_width = item_table.shape[1]
    shard_rows = item_table.shape[0]
    requests = fetch_rows.reshape(emb_count, -1)
    slot_count = requests.shape[0] * requests.shape[1]
    asked_rows = lax.all_to_all(requests, "emb", split_axis=0, concat_axis=0, tiled=True)
    found = item_table[asked_rows]
    fetched, asked_rows = (
        lax.all_to_all(found, "emb", split_axis=0, concat_axis=0, tiled=True),
        asked_rows,
    )
    slot_table = fetched.reshape(slot_count, model_width)
    events = slot_table[event_slot]
    lengths_row = lengths[0]

    def forward(rows_x, first, second):
        return hstu_layer(rows_x, first, second, lengths_row)

    layer_out, pullback = jax.vjp(forward, events, in_weight, out_weight)
    row_grad, first_grad, second_grad = pullback(out_grad)
    slot_grad = jax.ops.segment_sum(
        row_grad.astype(jnp.float32), event_slot, num_segments=slot_count
    )
    returned = lax.all_to_all(
        slot_grad.reshape(emb_count, -1, model_width).astype(jnp.bfloat16),
        "emb",
        split_axis=0,
        concat_axis=0,
        tiled=True,
    ).astype(jnp.float32)
    quarter = shard_rows // seq_count
    shared, shared_rows = (
        lax.all_gather(returned.astype(jnp.bfloat16), "seq", axis=0, tiled=True).astype(
            returned.dtype
        ),
        lax.all_gather(asked_rows, "seq", axis=0, tiled=True),
    )
    local_rows = shared_rows.reshape(-1) - lax.axis_index("seq") * quarter
    inside = (local_rows >= 0) & (local_rows < quarter)
    target = jnp.where(inside, local_rows, quarter)
    table_grad = jax.ops.segment_sum(
        shared.reshape(-1, model_width), target, num_segments=quarter + 1
    )[:quarter]
    in_total, out_total = lax.psum(
        (first_grad.astype(jnp.float32), second_grad.astype(jnp.float32)), ("emb", "seq")
    )
    return (layer_out, table_grad, in_total, out_total)


def solution(mesh):
    placed = (
        P("emb", None),
        P("emb", "seq", None, None),
        P(("emb", "seq")),
        P(("emb", "seq"), None),
        P(),
        P(),
        P(("emb", "seq"), None),
    )
    return jax.shard_map(
        on_device,
        mesh=mesh,
        in_specs=placed,
        out_specs=(P(("emb", "seq"), None), P(("emb", "seq"), None), P(), P()),
        check_vma=False,
    )
```

profile of v0, /device:TPU:0, one launch (start us, length us, event | category | flops | bytes accessed | tf_op | source)
XLA Modules:
  0.0 345.2 jit_solution(15317950688414619498)
XLA Ops:
  8.0 13.8 %all_to_all.25 = s32[8,1,64]{2,1,0:T(1,128)S(1)} all-to-all(s32[8,1,64]{2,1,0:T(1,128)} %bitcast.80), channel_id=1, replica_groups=mesh['emb'=8,'seq'=4] {'emb'}, dimensions={0} | all-to-all | bytes 4096 | tf_op jit(solution)/shard_map/all_to_all | solution.py:61
  22.0 5.4 %gather_fusion = bf16[512,512]{1,0:T(8,128)(2,1)} fusion(bf16[4096,512]{1,0:T(8,128)(2,1)} %param.7, s32[1024]{0:T(1024)S(1)} %pad_clamp_fusion), kind=kCustom, calls=%fused_computation | custom fusion | bytes 1050624 | tf_op jit(solution)/shard_map/gather | solution.py:62
  27.3 3.5 %all-to-all-start.1 = ((bf16[8,64,512]{2,1,0:T(8,128)(2,1)}), bf16[8,64,512]{2,1,0:T(8,128)(2,1)S(1)}, u32[]{:S(2)}, u32[]{:S(2)}) async-start(bf16[8,64,512]{2,1,0:T(8,128)(2,1)} %bitcast.2), calls=%async_computation.1 | async-start | bytes 1048576 | tf_op jit(solution)/shard_map/all_to_all | solution.py:64
  30.9 0.2 reduce-window.8
  31.1 0.1 convert_reduce_fusion.1
  31.2 1.6 fusion.8
  32.8 11.3 %all-to-all-done.1 = bf16[8,64,512]{2,1,0:T(8,128)(2,1)S(1)} async-done(((bf16[8,64,512]{2,1,0:T(8,128)(2,1)}), bf16[8,64,512]{2,1,0:T(8,128)(2,1)S(1)}, u32[]{:S(2)}, u32[]{:S(2)}) %all-to-all-start.1) | async-done | bytes 524320 | tf_op jit(solution)/shard_map/all_to_all | solution.py:64
  44.1 5.3 %gather_fusion.1 = bf16[1024,512]{1,0:T(8,128)(2,1)} fusion(bf16[512,512]{1,0:T(8,128)(2,1)S(1)} %bitcast.63, s32[1024]{0:T(1024)S(1)} %fusion.37), kind=kCustom, calls=%fused_computation.1 | custom fusion | bytes 2101248 | tf_op jit(solution)/shard_map/gather | solution.py:68
  49.4 1.4 convert_reduce_fusion
  50.9 1.7 fusion.14
  52.6 8.6 %fusion.44 = (bf16[1024,2048]{1,0:T(8,128)(2,1)S(1)}, f32[1024,2048]{1,0:T(8,128)}, f32[1024,2048]{1,0:T(8,128)}) fusion(bf16[512,2048]{1,0:T(8,128)(2,1)S(1)} %copy-done, bf16[1024,512]{1,0:T(8,128)(2,1)} %gather_fusion.1, f32[1024]{0:T(1024)S(1)} %fusion.38, f32[1024]{0:T(1024)S(1)} %broadcast_multiply_fusion.1), kind=kOutput, calls=%fused_computation.87 | convolution fusion | flops 2160066560 | bytes 24125440 | tf_op jit(solution)/shard_map/jvp()/dot_general | solution.py:21
  61.2 1.7 slice_bitcast_fusion
  62.9 2.3 copy.89
  65.2 1.3 copy.90
  66.5 11.8 %select_convert_fusion = (bf16[4,1024,1024]{2,1,0:T(8,128)(2,1)S(1)}, f32[4,1024,1024]{2,1,0:T(8,128)}) fusion(pred[1024,1024]{1,0:T(8,128)(4,1)} %fusion.8, bf16[1024,4,128]{0,2,1:T(8,128)(2,1)} %bitcast.72, bf16[1024,4,128]{0,2,1:T(8,128)(2,1)} %bitcast.74), kind=kOutput, calls=%fused_computation.8 | convolution fusion | flops 1107296256 | bytes 28311552 | tf_op jit(solution)/shard_map/jvp(ihd,jhd->hij)/dot_general | solution.py:36
  78.3 2.9 fusion.46
  81.2 0.3 copy-done.2
  81.5 1.3 copy-done.6
  82.8 0.3 fusion.19
  83.1 2.9 copy.84
  86.0 3.4 multiply_reduce_fusion
  89.4 3.6 %fusion.43 = (f32[1024]{0:T(1024)S(1)}, f32[1024,512]{1,0:T(8,128)S(1)}, bf16[1024,512]{1,0:T(8,128)(2,1)}, f32[1024,512]{1,0:T(8,128)}) fusion(f32[1024]{0:T(1024)S(1)} %get-tuple-element.15, f32[1024,512]{1,0:T(8,128)S(1)} %copy-done.5, f32[1024]{0:T(1024)S(1)} %broadcast_multiply_fusion, f32[1024]{0:T(1024)S(1)} %get-tuple-element.16, ...), kind=kLoop, calls=%fused_computation.86 | loop fusion | flops 6290432 | bytes 10502144 | tf_op jit(solution)/shard_map/transpose(jvp())/reduce_sum | solution.py:12
  93.1 1.2 broadcast_add_fusion
  94.3 1.5 copy.85
  95.8 15.3 %fusion.2 = bf16[4,1024,1024]{2,1,0:T(8,128)(2,1)} fusion(f32[4,1024,1024]{2,1,0:T(8,128)} %get-tuple-element.19, pred[1024,1024]{1,0:T(8,128)(4,1)} %fusion.8, bf16[4,128,1024]{2,1,0:T(8,128)(2,1)S(1)} %bitcast.67, bf16[128,4,8,128]{3,2,1,0:T(8,128)(2,1)} %get-tuple-element.11), kind=kOutput, calls=%fused_computation.7 | convolution fusion | flops 1136656384 | bytes 28311552 | tf_op jit(solution)/shard_map/transpose(jvp(hij,jhd->ihd))/dot_general | solution.py:44
  111.0 5.8 %fusion.49 = bf16[4,1024,128]{1,2,0:T(8,128)(2,1)} fusion(bf16[4,1024,1024]{2,1,0:T(8,128)(2,1)} %fusion.2, bf16[1024,4,128]{0,2,1:T(8,128)(2,1)S(1)} %bitcast.73), kind=kOutput, calls=%fused_computation.91 | convolution fusion | flops 1073741824 | bytes 10485760 | tf_op jit(solution)/shard_map/transpose(jvp(ihd,jhd->hij))/dot_general | solution.py:36
  116.9 7.5 %fusion.48 = bf16[4,1024,128]{1,2,0:T(8,128)(2,1)} fusion(bf16[4,1024,1024]{2,1,0:T(8,128)(2,1)} %fusion.2, bf16[1024,4,128]{0,2,1:T(8,128)(2,1)S(1)} %bitcast.75), kind=kOutput, calls=%fused_computation.90 | convolution fusion | flops 1073741824 | bytes 10485760 | tf_op jit(solution)/shard_map/transpose(jvp(ihd,jhd->hij))/dot_general | solution.py:36
  124.4 2.3 fusion.47
  126.7 2.4 copy.86
  129.1 2.3 copy.87
  131.4 1.3 copy.88
  132.7 7.1 %fusion.4 = bf16[1024,2048]{1,0:T(8,128)(2,1)S(1)} fusion(f32[1024,2048]{1,0:T(8,128)} %get-tuple-element.17, f32[1024,512]{1,0:T(8,128)} %get-tuple-element.14, bf16[1024,512]{1,0:T(8,128)(2,1)} %copy.88, bf16[1024,512]{1,0:T(8,128)(2,1)} %copy.87, bf16[1024,512]{1,0:T(8,128)(2,1)} %copy.86), kind=kLoop, calls=%fused_computation.12 | loop fusion | flops 33554432 | bytes 17825792 | tf_op jit(solution)/shard_map/transpose(jvp(jit(silu)))/add_any | solution.py:21
  139.8 2.5 fusion.16
  142.3 0.9 copy-done.7
  143.3 1.0 fusion.22
  144.3 9.1 %scatter_custom_fusion = f32[512,512]{1,0:T(8,128)} fusion(s32[1024]{0:T(1024)S(1)} %copy-done.14, bf16[1024,512]{1,0:T(8,128)(2,1)} %param.13, bf16[1024,512]{1,0:T(8,128)(2,1)S(1)} %copy-done.1, bf16[1024,512]{1,0:T(8,128)(2,1)} %copy-done.7, f32[1024]{0:T(1024)S(1)} %negate_multiply_fusion, f32[1024]{0:T(1024)S(1)} %multiply_multiply_fusion, ...), kind=kCustom, calls=%fused_computation.40 | custom fusion | flops 6291456 | bytes 4210692 | tf_op jit(solution)/shard_map/scatter-add | solution.py:76
  153.4 1.3 convert_element_type.125
  154.7 17.4 %all_to_all.26 = bf16[8,64,512]{2,1,0:T(8,128)(2,1)} all-to-all(bf16[8,64,512]{2,1,0:T(8,128)(2,1)S(1)} %bitcast.70), channel_id=1, replica_groups=mesh['emb'=8,'seq'=4] {'emb'}, dimensions={0} | all-to-all | bytes 1048576 | tf_op jit(solution)/shard_map/all_to_all | solution.py:79
  172.1 3.4 fusion.23
  175.5 4.6 %fusion.13 = f32[512,2048]{1,0:T(8,128)} fusion(bf16[1024,2048]{1,0:T(8,128)(2,1)S(1)} %copy-done.4, bf16[1024,512]{1,0:T(8,128)(2,1)S(1)} %copy-done.1, f32[1024]{0:T(1024)S(1)} %fusion.38, f32[1024]{0:T(1024)S(1)} %broadcast_multiply_fusion.1), kind=kOutput, calls=%fused_computation.29 | convolution fusion | flops 2150629376 | bytes 9445376 | tf_op jit(solution)/shard_map/transpose(jvp())/dot_general | solution.py:21
  180.2 5.4 %all-gather = s32[32,1,64]{2,1,0:T(1,128)S(1)} all-gather(s32[8,1,64]{2,1,0:T(1,128)S(1)} %all_to_all.25), channel_id=2, replica_groups=mesh['emb'=8,'seq'=4] {'seq'}, dimensions={0}, use_global_device_ids=true | all-gather | bytes 10240 | tf_op jit(solution)/shard_map/all_gather | solution.py:91
  185.7 3.1 fusion.17
  188.8 5.5 %all-gather.3.cloned.1.call-done = bf16[32,64,512]{2,1,0:T(8,128)(2,1)} async-done(((bf16[8,64,512]{2,1,0:T(8,128)(2,1)}), bf16[32,64,512]{2,1,0:T(8,128)(2,1)}) %all-gather.3.cloned.1.call-update) | async-done | bytes 2097168 | tf_op jit(solution)/shard_map/all_gather | solution.py:88
  194.3 15.0 %scatter_custom_fusion.1 = f32[1025,512]{1,0:T(8,128)} fusion(s32[2048]{0:T(1024)S(1)} %bitcast.79, bf16[2048,512]{1,0:T(8,128)(2,1)} %bitcast.71, f32[]{:T(128)} %constant.22.clone.1), kind=kCustom, calls=%fused_computation.15 | custom fusion | flops 2097152 | bytes 4196356 | tf_op jit(solution)/shard_map/scatter-add | solution.py:96
  209.3 3.1 slice.31
  212.4 119.4 %all-reduce.7.cloned.1.call-done = (f32[512,2048]{1,0:T(8,128)}, f32[512,512]{1,0:T(8,128)}) async-done(((f32[512,2048]{1,0:T(8,128)}, f32[512,512]{1,0:T(8,128)}), (f32[512,2048]{1,0:T(8,128)}, f32[512,512]{1,0:T(8,128)})) %all-reduce.7.cloned.1.call-update) | async-done | bytes 5242896 | tf_op jit(solution)/shard_map/psum | solution.py:99
  331.8 4.8 %copy.104 = f32[512,2048]{1,0:T(8,128)} copy(f32[512,2048]{1,0:T(8,128)} %get-tuple-element.28) | data formatting | bytes 8388608
  336.6 1.0 copy.105
  (52 shorter events, 0.5 us)
Async XLA Ops:
  8.0 44.6 %copy-start = (bf16[512,2048]{1,0:T(8,128)(2,1)S(1)}, bf16[512,2048]{1,0:T(8,128)(2,1)}, u32[]{:S(2)}) copy-start(bf16[512,2048]{1,0:T(8,128)(2,1)} %param.11) | copy-start | bytes 6291460
  8.0 22.9 %copy-start.15 = (s32[1,8]{1,0:T(1,128)S(1)}, s32[1,8]{1,0:T(1,128)}, u32[]{:S(2)}) copy-start(s32[1,8]{1,0:T(1,128)} %param.10) | copy-start | bytes 100
  8.0 23.2 %copy-start.14 = (s32[1024]{0:T(1024)S(1)}, s32[1024]{0:T(1024)}, u32[]{:S(2)}) copy-start(s32[1024]{0:T(1024)} %param.9) | copy-start | bytes 12292
  27.3 16.8 %all-to-all-start.1 = ((bf16[8,64,512]{2,1,0:T(8,128)(2,1)}), bf16[8,64,512]{2,1,0:T(8,128)(2,1)S(1)}, u32[]{:S(2)}, u32[]{:S(2)}) async-start(bf16[8,64,512]{2,1,0:T(8,128)(2,1)} %bitcast.2), calls=%async_computation.1 | async-start | bytes 1048576 | tf_op jit(solution)/shard_map/all_to_all | solution.py:64
  30.8 163.4 %all-gather.3.cloned.1.call-start = ((), (), s32[]{:S(2)}) async-start(), calls=%async_computation.3 | async-start | bytes 2621440 | tf_op jit(solution)/shard_map/all_gather | solution.py:88
  66.5 11.8 %copy-start.10 = (bf16[128,4,8,128]{3,2,1,0:T(8,128)(2,1)S(1)}, bf16[128,4,8,128]{3,2,1,0:T(8,128)(2,1)}, u32[]{:S(2)}) copy-start(bf16[128,4,8,128]{3,2,1,0:T(8,128)(2,1)} %get-tuple-element.11) | copy-start | bytes 3145732
  78.3 3.2 copy-start.2
  81.5 1.3 copy-start.6
  81.5 4.5 %copy-start.9 = (bf16[1024,512]{1,0:T(8,128)(2,1)S(1)}, bf16[1024,512]{1,0:T(8,128)(2,1)}, u32[]{:S(2)}) copy-start(bf16[1024,512]{1,0:T(8,128)(2,1)} %param.13) | copy-start | bytes 3145732
  86.0 3.4 copy-start.5
  95.8 15.3 %copy-start.11 = (bf16[1024,512]{0,1:T(8,128)(2,1)S(1)}, bf16[1024,512]{0,1:T(8,128)(2,1)}, u32[]{:S(2)}) copy-start(bf16[1024,512]{0,1:T(8,128)(2,1)} %copy.89) | copy-start | bytes 3145732
  111.0 5.8 %copy-start.12 = (bf16[1024,512]{0,1:T(8,128)(2,1)S(1)}, bf16[1024,512]{0,1:T(8,128)(2,1)}, u32[]{:S(2)}) copy-start(bf16[1024,512]{0,1:T(8,128)(2,1)} %copy.90) | copy-start | bytes 3145732
  111.0 13.3 %slice-start = ((s8[8388608]{0:T(1024)(128)(4,1)}), s8[4194304]{0:T(1024)(128)(4,1)S(1)}, s32[]{:S(2)}) async-start(s8[8388608]{0:T(1024)(128)(4,1)} %bitcast.64), calls=%async_computation.5 | async-start | bytes 8388608
  116.9 7.5 %slice-start.1 = ((s8[8388608]{0:T(1024)(128)(4,1)}), s8[4194304]{0:T(1024)(128)(4,1)S(1)}, s32[]{:S(2)}) async-start(s8[8388608]{0:T(1024)(128)(4,1)} %bitcast.64), calls=%async_computation.6 | async-start | bytes 8388608
  126.7 4.7 %copy-start.8 = (bf16[4,128,1024]{2,1,0:T(8,128)(2,1)S(1)}, bf16[4,128,1024]{2,1,0:T(8,128)(2,1)}, u32[]{:S(2)}) copy-start(bf16[4,128,1024]{2,1,0:T(8,128)(2,1)} %fusion.47) | copy-start | bytes 3145732
  132.7 7.1 %copy-start.1 = (bf16[1024,512]{1,0:T(8,128)(2,1)S(1)}, bf16[1024,512]{1,0:T(8,128)(2,1)}, u32[]{:S(2)}) copy-start(bf16[1024,512]{1,0:T(8,128)(2,1)} %gather_fusion.1) | copy-start | bytes 3145732
  139.8 2.5 copy-start.3
  142.3 1.0 copy-start.7
  172.1 159.7 %all-reduce.7.cloned.1.call-start = ((), (), s32[]{:S(2)}) async-start(), calls=%async_computation.4 | async-start | bytes 10485760 | tf_op jit(solution)/shard_map/psum | solution.py:99
  172.1 3.4 copy-start.4
  331.8 4.8 %copy-start.13 = (f32[512,512]{1,0:T(8,128)S(1)}, f32[512,512]{1,0:T(8,128)}, u32[]{:S(2)}) copy-start(f32[512,512]{1,0:T(8,128)} %get-tuple-element.29) | copy-start | bytes 3145732
Sparse Core Ops, SparseCore 0:
  172.2 22.0 all-gather.2
Sparse Core Ops, SparseCore 1:
  180.3 151.5 all-reduce.6
where the time goes:
time: 348 us; the launch traced here: 345 us
  waiting for transfers between devices  136 us (39%)
  matrix products  71.2 us (20%)
  other arithmetic  43.7 us (13%)
  local copies, waits for them, and re-layouts  38 us (11%)
  blocking collectives  36.6 us (11%)
  between operations  15.9 us (5%)
  starting transfers between devices  3.58 us (1%)
    psum x1, waiting for transfers between devices, on_device(): lax.psum((first_grad.astype(jnp.float32), second_grad.astype(jnp.float32)...  119 us
    dot_general x3, matrix products, hstu_layer(): jnp.einsum('ihd,jhd->hij', queries, key_rows, preferred_element_type=jnp....  25.1 us
    dot_general x3, matrix products, hstu_layer(): jnp.einsum('hij,jhd->ihd', weights, values, preferred_element_type=jnp.fl...  20.5 us
    all_to_all x1, blocking collectives, on_device(): lax.all_to_all(slot_grad.reshape(emb_count, -1, model_width).astype(jnp.b...  17.4 us
    dot_general x3, matrix products, hstu_layer(): jnp.dot(normed, in_weight, preferred_element_type=jnp.float32)  15.7 us
    scatter-add x1, other arithmetic, on_device(): jax.ops.segment_sum(shared.reshape(-1, model_width), target, num_segments...  15 us
    all_to_all x1, blocking collectives, on_device(): lax.all_to_all(requests, 'emb', split_axis=0, concat_axis=0, tiled=True)  13.8 us
    all_to_all x1, waiting for transfers between devices, on_device(): lax.all_to_all(found, 'emb', split_axis=0, concat_axis=0, tiled=True)  11.3 us
  transfers between devices with their start and end apart: 3, of which 3 were waited for; matrix products, arithmetic and copies ran while one was open for 9% of the time, Pallas kernels for 0%

commit v1 on v0

--- a/solution.py
+++ b/solution.py
@@ -97,7 +97,7 @@
         shared.reshape(-1, model_width), target, num_segments=quarter + 1
     )[:quarter]
     in_total, out_total = lax.psum(
-        (first_grad.astype(jnp.float32), second_grad.astype(jnp.float32)), ("emb", "seq")
+        lax.psum((first_grad.astype(jnp.float32), second_grad.astype(jnp.float32)), "seq"), "emb"
     )
     return (layer_out, table_grad, in_total, out_total)
 

time: 348 us -> 474 us (1.36)
  waiting for transfers between devices: 136 us -> 264 us
    psum x0 -> x1, waiting for transfers between devices: none -> 170 us  [on_device(): lax.psum(lax.psum((first_grad.astype(jnp.float32), second_grad.astype(jnp...]
    psum x1, waiting for transfers between devices: 119 us -> 66.8 us  [on_device(): lax.psum((first_grad.astype(jnp.float32), second_grad.astype(jnp.float32)...]
    all_gather x1, waiting for transfers between devices: 5.5 us -> 15.9 us  [on_device(): lax.all_gather(returned.astype(jnp.bfloat16), 'seq', axis=0, tiled=True)]
    unnamed x39 -> x41, local copies, waits for them, and re-layouts: 10.1 us -> 10.1 us
  transfers between devices with their start and end apart: 3 -> 4, of which waited for: 3 -> 4; matrix products, arithmetic and copies ran while one was open for 9% -> 8% of each run, Pallas kernels for 0% -> 0%
where the time goes in v1:
time: 474 us; the launch traced here: 471 us
  waiting for transfers between devices  264 us (56%)
  matrix products  71.3 us (15%)
  other arithmetic  43.3 us (9%)
  local copies, waits for them, and re-layouts  38.1 us (8%)
  blocking collectives  36.7 us (8%)
  between operations  14.2 us (3%)
    psum x1, waiting for transfers between devices, on_device(): lax.psum(lax.psum((first_grad.astype(jnp.float32), second_grad.astype(jnp...  170 us
    psum x1, waiting for transfers between devices, on_device(): lax.psum((first_grad.astype(jnp.float32), second_grad.astype(jnp.float32)...  66.8 us
    dot_general x3, matrix products, hstu_layer(): jnp.einsum('ihd,jhd->hij', queries, key_rows, preferred_element_type=jnp....  25.1 us
    dot_general x3, matrix products, hstu_layer(): jnp.einsum('hij,jhd->ihd', weights, values, preferred_element_type=jnp.fl...  20.2 us
    dot_general x3, matrix products, hstu_layer(): jnp.dot(normed, in_weight, preferred_element_type=jnp.float32)  17.8 us
    all_to_all x1, blocking collectives, on_device(): lax.all_to_all(slot_grad.reshape(emb_count, -1, model_width).astype(jnp.b...  17.6 us
    all_gather x1, waiting for transfers between devices, on_device(): lax.all_gather(returned.astype(jnp.bfloat16), 'seq', axis=0, tiled=True)  15.9 us
    scatter-add x1, other arithmetic, on_device(): jax.ops.segment_sum(shared.reshape(-1, model_width), target, num_segments...  14.8 us
  transfers between devices with their start and end apart: 4, of which 4 were waited for; matrix products, arithmetic and copies ran while one was open for 8% of the time, Pallas kernels for 0%

profile of v1, /device:TPU:0, one launch (start us, length us, event | category | flops | bytes accessed | tf_op | source)
XLA Modules:
  0.0 471.2 jit_solution(5368366663374485112)
XLA Ops:
  7.2 13.8 %all_to_all.25 = s32[8,1,64]{2,1,0:T(1,128)S(1)} all-to-all(s32[8,1,64]{2,1,0:T(1,128)} %bitcast.80), channel_id=1, replica_groups=mesh['emb'=8,'seq'=4] {'emb'}, dimensions={0} | all-to-all | bytes 4096 | tf_op jit(solution)/shard_map/all_to_all | solution.py:61
  21.1 5.4 %gather_fusion = bf16[512,512]{1,0:T(8,128)(2,1)} fusion(bf16[4096,512]{1,0:T(8,128)(2,1)} %param.7, s32[1024]{0:T(1024)S(1)} %pad_clamp_fusion), kind=kCustom, calls=%fused_computation | custom fusion | bytes 1050624 | tf_op jit(solution)/shard_map/gather | solution.py:62
  26.5 3.5 all-to-all-start.1
  30.4 1.6 fusion.8
  31.9 11.3 %all-to-all-done.1 = bf16[8,64,512]{2,1,0:T(8,128)(2,1)S(1)} async-done(((bf16[8,64,512]{2,1,0:T(8,128)(2,1)}), bf16[8,64,512]{2,1,0:T(8,128)(2,1)S(1)}, u32[]{:S(2)}, u32[]{:S(2)}) %all-to-all-start.1) | async-done | bytes 524320 | tf_op jit(solution)/shard_map/all_to_all | solution.py:64
  43.3 5.5 %gather_fusion.1 = bf16[1024,512]{1,0:T(8,128)(2,1)} fusion(bf16[512,512]{1,0:T(8,128)(2,1)S(1)} %bitcast.63, s32[1024]{0:T(1024)S(1)} %fusion.37), kind=kCustom, calls=%fused_computation.1 | custom fusion | bytes 2101248 | tf_op jit(solution)/shard_map/gather | solution.py:68
  48.8 1.4 convert_reduce_fusion
  50.2 1.7 fusion.14
  52.0 8.6 %fusion.44 = (bf16[1024,2048]{1,0:T(8,128)(2,1)S(1)}, f32[1024,2048]{1,0:T(8,128)}, f32[1024,2048]{1,0:T(8,128)}) fusion(bf16[512,2048]{1,0:T(8,128)(2,1)S(1)} %copy-done, bf16[1024,512]{1,0:T(8,128)(2,1)} %gather_fusion.1, f32[1024]{0:T(1024)S(1)} %fusion.38, f32[1024]{0:T(1024)S(1)} %broadcast_multiply_fusion.1), kind=kOutput, calls=%fused_computation.87 | convolution fusion | flops 2160066560 | bytes 24125440 | tf_op jit(solution)/shard_map/jvp()/dot_general | solution.py:21
  60.6 1.7 slice_bitcast_fusion
  62.3 2.3 copy.89
  64.5 1.3 copy.90
  65.9 11.8 %select_convert_fusion = (bf16[4,1024,1024]{2,1,0:T(8,128)(2,1)S(1)}, f32[4,1024,1024]{2,1,0:T(8,128)}) fusion(pred[1024,1024]{1,0:T(8,128)(4,1)} %fusion.8, bf16[1024,4,128]{0,2,1:T(8,128)(2,1)} %bitcast.72, bf16[1024,4,128]{0,2,1:T(8,128)(2,1)} %bitcast.74), kind=kOutput, calls=%fused_computation.8 | convolution fusion | flops 1107296256 | bytes 28311552 | tf_op jit(solution)/shard_map/jvp(ihd,jhd->hij)/dot_general | solution.py:36
  77.6 2.9 fusion.46
  80.6 0.3 copy-done.2
  80.8 1.3 copy-done.5
  82.2 0.3 fusion.19
  82.5 2.9 copy.84
  85.3 3.4 multiply_reduce_fusion
  88.8 3.6 fusion.43
  92.4 1.2 broadcast_add_fusion
  93.6 1.5 copy.85
  95.1 15.0 %fusion.2 = bf16[4,1024,1024]{2,1,0:T(8,128)(2,1)} fusion(f32[4,1024,1024]{2,1,0:T(8,128)} %get-tuple-element.21, pred[1024,1024]{1,0:T(8,128)(4,1)} %fusion.8, bf16[4,128,1024]{2,1,0:T(8,128)(2,1)S(1)} %bitcast.67, bf16[128,4,8,128]{3,2,1,0:T(8,128)(2,1)} %get-tuple-element.13), kind=kOutput, calls=%fused_computation.7 | convolution fusion | flops 1136656384 | bytes 28311552 | tf_op jit(solution)/shard_map/transpose(jvp(hij,jhd->ihd))/dot_general | solution.py:44
  110.1 5.8 %fusion.49 = bf16[4,1024,128]{1,2,0:T(8,128)(2,1)} fusion(bf16[4,1024,1024]{2,1,0:T(8,128)(2,1)} %fusion.2, bf16[1024,4,128]{0,2,1:T(8,128)(2,1)S(1)} %bitcast.73), kind=kOutput, calls=%fused_computation.91 | convolution fusion | flops 1073741824 | bytes 10485760 | tf_op jit(solution)/shard_map/transpose(jvp(ihd,jhd->hij))/dot_general | solution.py:36
  116.0 7.5 %fusion.48 = bf16[4,1024,128]{1,2,0:T(8,128)(2,1)} fusion(bf16[4,1024,1024]{2,1,0:T(8,128)(2,1)} %fusion.2, bf16[1024,4,128]{0,2,1:T(8,128)(2,1)S(1)} %bitcast.75), kind=kOutput, calls=%fused_computation.90 | convolution fusion | flops 1073741824 | bytes 10485760 | tf_op jit(solution)/shard_map/transpose(jvp(ihd,jhd->hij))/dot_general | solution.py:36
  123.5 2.3 fusion.47
  125.8 2.4 copy.86
  128.2 2.3 copy.87
  130.5 1.3 copy.88
  131.8 7.0 %fusion.4 = bf16[1024,2048]{1,0:T(8,128)(2,1)S(1)} fusion(f32[1024,2048]{1,0:T(8,128)} %get-tuple-element.19, f32[1024,512]{1,0:T(8,128)} %get-tuple-element.16, bf16[1024,512]{1,0:T(8,128)(2,1)} %copy.88, bf16[1024,512]{1,0:T(8,128)(2,1)} %copy.87, bf16[1024,512]{1,0:T(8,128)(2,1)} %copy.86), kind=kLoop, calls=%fused_computation.12 | loop fusion | flops 33554432 | bytes 17825792 | tf_op jit(solution)/shard_map/transpose(jvp(jit(silu)))/add_any | solution.py:21
  138.8 4.5 fusion.13
  143.3 1.7 fusion.23
  145.0 0.3 all-gather.3.cloned.1.call-start
  145.3 4.6 fusion.16
  149.9 0.9 copy-done.6
  150.9 1.0 fusion.22
  151.9 9.1 %scatter_custom_fusion = f32[512,512]{1,0:T(8,128)} fusion(s32[1024]{0:T(1024)S(1)} %copy-done.15, bf16[1024,512]{1,0:T(8,128)(2,1)} %param.13, bf16[1024,512]{1,0:T(8,128)(2,1)S(1)} %copy-done.1, bf16[1024,512]{1,0:T(8,128)(2,1)} %copy-done.6, f32[1024]{0:T(1024)S(1)} %negate_multiply_fusion, f32[1024]{0:T(1024)S(1)} %multiply_multiply_fusion, ...), kind=kCustom, calls=%fused_computation.40 | custom fusion | flops 6291456 | bytes 4210692 | tf_op jit(solution)/shard_map/scatter-add | solution.py:76
  161.0 1.3 convert_element_type.125
  162.3 17.6 %all_to_all.26 = bf16[8,64,512]{2,1,0:T(8,128)(2,1)} all-to-all(bf16[8,64,512]{2,1,0:T(8,128)(2,1)S(1)} %bitcast.70), channel_id=1, replica_groups=mesh['emb'=8,'seq'=4] {'emb'}, dimensions={0} | all-to-all | bytes 1048576 | tf_op jit(solution)/shard_map/all_to_all | solution.py:79
  180.0 66.8 %all-reduce.11.cloned.1.call-done = (f32[512,2048]{1,0:T(8,128)}, f32[512,512]{1,0:T(8,128)}) async-done(((f32[512,2048]{1,0:T(8,128)}, f32[512,512]{1,0:T(8,128)}), (f32[512,2048]{1,0:T(8,128)}, f32[512,512]{1,0:T(8,128)})) %all-reduce.11.cloned.1.call-update) | async-done | bytes 5242896 | tf_op jit(solution)/shard_map/psum | solution.py:100
  246.9 5.2 %all-gather = s32[32,1,64]{2,1,0:T(1,128)S(1)} all-gather(s32[8,1,64]{2,1,0:T(1,128)S(1)} %all_to_all.25), channel_id=2, replica_groups=mesh['emb'=8,'seq'=4] {'seq'}, dimensions={0}, use_global_device_ids=true | all-gather | bytes 10240 | tf_op jit(solution)/shard_map/all_gather | solution.py:91
  252.2 3.0 fusion.17
  255.2 15.9 %all-gather.3.cloned.1.call-done = bf16[32,64,512]{2,1,0:T(8,128)(2,1)} async-done(((bf16[8,64,512]{2,1,0:T(8,128)(2,1)}), bf16[32,64,512]{2,1,0:T(8,128)(2,1)}) %all-gather.3.cloned.1.call-update) | async-done | bytes 2097168 | tf_op jit(solution)/shard_map/all_gather | solution.py:88
  271.1 14.8 %scatter_custom_fusion.1 = f32[1025,512]{1,0:T(8,128)} fusion(s32[2048]{0:T(1024)S(1)} %bitcast.79, bf16[2048,512]{1,0:T(8,128)(2,1)} %bitcast.71, f32[]{:T(128)} %constant.22.clone.1), kind=kCustom, calls=%fused_computation.15 | custom fusion | flops 2097152 | bytes 4196356 | tf_op jit(solution)/shard_map/scatter-add | solution.py:96
  285.9 3.1 slice.31
  289.0 169.7 %all-reduce.9.cloned.1.call-done = (f32[512,2048]{1,0:T(8,128)}, f32[512,512]{1,0:T(8,128)}) async-done(((f32[512,2048]{1,0:T(8,128)}, f32[512,512]{1,0:T(8,128)}), (f32[512,2048]{1,0:T(8,128)}, f32[512,512]{1,0:T(8,128)})) %all-reduce.9.cloned.1.call-update) | async-done | bytes 5242896 | tf_op jit(solution)/shard_map/psum | solution.py:99
  458.7 4.8 %copy.106 = f32[512,2048]{1,0:T(8,128)} copy(f32[512,2048]{1,0:T(8,128)} %get-tuple-element.30) | data formatting | bytes 8388608
  463.5 1.0 copy.107
  (57 shorter events, 0.8 us)
Async XLA Ops:
  7.2 44.8 %copy-start = (bf16[512,2048]{1,0:T(8,128)(2,1)S(1)}, bf16[512,2048]{1,0:T(8,128)(2,1)}, u32[]{:S(2)}) copy-start(bf16[512,2048]{1,0:T(8,128)(2,1)} %param.11) | copy-start | bytes 6291460
  7.2 22.9 %copy-start.16 = (s32[1,8]{1,0:T(1,128)S(1)}, s32[1,8]{1,0:T(1,128)}, u32[]{:S(2)}) copy-start(s32[1,8]{1,0:T(1,128)} %param.10) | copy-start | bytes 100
  7.2 23.2 %copy-start.15 = (s32[1024]{0:T(1024)S(1)}, s32[1024]{0:T(1024)}, u32[]{:S(2)}) copy-start(s32[1024]{0:T(1024)} %param.9) | copy-start | bytes 12292
  26.5 16.8 %all-to-all-start.1 = ((bf16[8,64,512]{2,1,0:T(8,128)(2,1)}), bf16[8,64,512]{2,1,0:T(8,128)(2,1)S(1)}, u32[]{:S(2)}, u32[]{:S(2)}) async-start(bf16[8,64,512]{2,1,0:T(8,128)(2,1)} %bitcast.2), calls=%async_computation.1 | async-start | bytes 1048576 | tf_op jit(solution)/shard_map/all_to_all | solution.py:64
  30.0 216.8 %all-reduce.11.cloned.1.call-start = ((), (), s32[]{:S(2)}) async-start(), calls=%async_computation.5 | async-start | bytes 10485760 | tf_op jit(solution)/shard_map/psum | solution.py:100
  65.9 11.8 %copy-start.10 = (bf16[128,4,8,128]{3,2,1,0:T(8,128)(2,1)S(1)}, bf16[128,4,8,128]{3,2,1,0:T(8,128)(2,1)}, u32[]{:S(2)}) copy-start(bf16[128,4,8,128]{3,2,1,0:T(8,128)(2,1)} %get-tuple-element.13) | copy-start | bytes 3145732
  77.6 3.2 copy-start.2
  80.8 1.3 copy-start.5
  80.8 4.5 copy-start.8
  85.3 3.4 copy-start.4
  95.1 15.0 %copy-start.12 = (bf16[1024,512]{0,1:T(8,128)(2,1)S(1)}, bf16[1024,512]{0,1:T(8,128)(2,1)}, u32[]{:S(2)}) copy-start(bf16[1024,512]{0,1:T(8,128)(2,1)} %copy.89) | copy-start | bytes 3145732
  110.1 5.8 %copy-start.13 = (bf16[1024,512]{0,1:T(8,128)(2,1)S(1)}, bf16[1024,512]{0,1:T(8,128)(2,1)}, u32[]{:S(2)}) copy-start(bf16[1024,512]{0,1:T(8,128)(2,1)} %copy.90) | copy-start | bytes 3145732
  110.1 13.3 %slice-start = ((s8[8388608]{0:T(1024)(128)(4,1)}), s8[4194304]{0:T(1024)(128)(4,1)S(1)}, s32[]{:S(2)}) async-start(s8[8388608]{0:T(1024)(128)(4,1)} %bitcast.64), calls=%async_computation.6 | async-start | bytes 8388608
  116.0 7.5 %slice-start.1 = ((s8[8388608]{0:T(1024)(128)(4,1)}), s8[4194304]{0:T(1024)(128)(4,1)S(1)}, s32[]{:S(2)}) async-start(s8[8388608]{0:T(1024)(128)(4,1)} %bitcast.64), calls=%async_computation.7 | async-start | bytes 8388608
  125.8 4.7 copy-start.7
  131.8 7.0 %copy-start.1 = (bf16[1024,512]{1,0:T(8,128)(2,1)S(1)}, bf16[1024,512]{1,0:T(8,128)(2,1)}, u32[]{:S(2)}) copy-start(bf16[1024,512]{1,0:T(8,128)(2,1)} %gather_fusion.1) | copy-start | bytes 3145732
  138.8 4.5 copy-start.3
  138.8 4.5 copy-start.9
  138.8 4.5 copy-start.11
  145.0 126.1 %all-gather.3.cloned.1.call-start = ((), (), s32[]{:S(2)}) async-start(), calls=%async_computation.3 | async-start | bytes 2621440 | tf_op jit(solution)/shard_map/all_gather | solution.py:88
  149.9 1.0 copy-start.6
  180.0 278.7 %all-reduce.9.cloned.1.call-start = ((), (), s32[]{:S(2)}) async-start(), calls=%async_computation.4 | async-start | bytes 10485760 | tf_op jit(solution)/shard_map/psum | solution.py:99
  458.7 4.8 %copy-start.14 = (f32[512,512]{1,0:T(8,128)S(1)}, f32[512,512]{1,0:T(8,128)}, u32[]{:S(2)}) copy-start(f32[512,512]{1,0:T(8,128)} %get-tuple-element.31) | copy-start | bytes 3145732
Sparse Core Ops, SparseCore 0:
  145.1 101.6 all-reduce.10
  248.4 22.7 all-gather.2
  274.9 183.8 all-reduce.8
